TPU v7x, 32 devices: a whole 2x2x4 slice. The times are simulated.
32 devices in a mesh: seq: 4 (over x, core), fsdp: 8 (over z, y).
Axes of the slice: x: 2, y: 2, z: 4, core: 2. Of those that a mesh axis runs over, the one named last changes fastest.
Arguments:
- tokens: bfloat16 [8, 1024, 2048], P('fsdp', 'seq'), may hold values from -6 to 6
- targets: bfloat16 [8, 1024, 2048], P('fsdp', 'seq'), may hold values from -6 to 6
- lengths: int32 [8], replicated, may hold values from 1 to 1024, 6144 in all
- w_qkv: float32 [2048, 3, 2048], P('fsdp', None, 'seq'), may hold values from -0.125 to 0.125
- w_out: float32 [2048, 2048], P('seq', 'fsdp'), may hold values from -1 to 1
- w_gateup: float32 [2048, 2, 8192], P('fsdp', None, 'seq'), may hold values from -0.125 to 0.125
- w_down: float32 [8192, 2048], P('seq', 'fsdp'), may hold values from -0.0625 to 0.0625
- mom_qkv: float32 [2048, 3, 2048], P('fsdp', None, 'seq'), may hold values from -0.0390625 to 0.0390625
- mom_out: float32 [2048, 2048], P('seq', 'fsdp'), may hold values from -0.0234375 to 0.0234375
- mom_gateup: float32 [2048, 2, 8192], P('fsdp', None, 'seq'), may hold values from -0.0390625 to 0.0390625
- mom_down: float32 [8192, 2048], P('seq', 'fsdp'), may hold values from -0.078125 to 0.078125
- avg_qkv: float32 [2048, 3, 2048], P('fsdp', None, 'seq'), may hold values from -0.125 to 0.125
- avg_out: float32 [2048, 2048], P('seq', 'fsdp'), may hold values from -1 to 1
- avg_gateup: float32 [2048, 2, 8192], P('fsdp', None, 'seq'), may hold values from -0.125 to 0.125
- avg_down: float32 [8192, 2048], P('seq', 'fsdp'), may hold values from -0.0625 to 0.0625
Outputs:
- output: bfloat16 [8, 1024, 2048], P('fsdp', 'seq')
- input_grad: bfloat16 [8, 1024, 2048], P('fsdp', 'seq')
- loss: float32 [], replicated
- new_qkv: float32 [2048, 3, 2048], P('fsdp', None, 'seq')
- new_out: float32 [2048, 2048], P('seq', 'fsdp')
- new_gateup: float32 [2048, 2, 8192], P('fsdp', None, 'seq')
- new_down: float32 [8192, 2048], P('seq', 'fsdp')
- newmom_qkv: float32 [2048, 3, 2048], P('fsdp', None, 'seq')
- newmom_out: float32 [2048, 2048], P('seq', 'fsdp')
- newmom_gateup: float32 [2048, 2, 8192], P('fsdp', None, 'seq')
- newmom_down: float32 [8192, 2048], P('seq', 'fsdp')
- newavg_qkv: float32 [2048, 3, 2048], P('fsdp', None, 'seq')
- newavg_out: float32 [2048, 2048], P('seq', 'fsdp')
- newavg_gateup: float32 [2048, 2, 8192], P('fsdp', None, 'seq')
- newavg_down: float32 [8192, 2048], P('seq', 'fsdp')
Inputs may be any that keep to these rules, and one draw needn't show every extreme that they name: lengths[s] valid tokens stand first in sequence s's 1024 slots, padding after; they sum to 6144 and one equals 1024.
All inputs are finite; a program needn't handle non-finite values.
Results may differ from a plain program's by a relative error of at most 0.015.
Values may be sent and summed in bfloat16 or wider, within the bound.
A program may use at most 256 MiB of HBM per device.

v0:
```python
import jax
import jax.numpy as jnp
from jax import lax
from jax.sharding import PartitionSpec as P

HD = 128
EPS = 1e-05
ROPE_BASE = 10000.0
MOMENT = 0.9
KEEP = 0.95
NEG = -1e30


def layer_norm(values):
    centred = values - jnp.mean(values, axis=-1, keepdims=True)
    factor = lax.rsqrt(jnp.mean(centred * centred, axis=-1, keepdims=True) + EPS)
    return (centred * factor, factor)


def norm_back(grad, normed, factor):
    inner = jnp.mean(grad * normed, axis=-1, keepdims=True)
    return factor * (grad - jnp.mean(grad, axis=-1, keepdims=True) - normed * inner)


def rotary(span, width):
    half = width // 2
    freq = ROPE_BASE ** (-2.0 * jnp.arange(half, dtype=jnp.float32) / width)
    angle = jnp.arange(span, dtype=jnp.float32)[:, None] * freq[None, :]
    cosine = jnp.concatenate([jnp.cos(angle), jnp.cos(angle)], axis=-1)[:, None, :]
    sine = jnp.concatenate([jnp.sin(angle), jnp.sin(angle)], axis=-1)[:, None, :]
    return (cosine, sine)


def rotate(values):
    half = values.shape[-1] // 2
    return jnp.concatenate([-values[..., half:], values[..., :half]], axis=-1)


def unrotate(values):
    half = values.shape[-1] // 2
    return jnp.concatenate([values[..., half:], -values[..., :half]], axis=-1)


def allowed_mask(first_row, block_rows, span, length):
    positions = jnp.arange(span, dtype=jnp.int32)
    query_pos = first_row + jnp.arange(block_rows, dtype=jnp.int32)
    return (positions[None, :] <= query_pos[:, None]) & (positions[None, :] < length)


def attend_forward(queries, keys_rot, values_v, length):
    span = queries.shape[0]
    block_rows = min(512, span)
    scale = queries.shape[2] ** (-0.5)

    def one_block(first_row):
        rows_q = lax.dynamic_slice_in_dim(queries, first_row, block_rows, 0)
        scores = (
            jnp.einsum("qhd,khd->hqk", rows_q, keys_rot, preferred_element_type=jnp.float32) * scale
        )
        scores = jnp.where(allowed_mask(first_row, block_rows, span, length)[None], scores, NEG)
        highest = jnp.max(scores, axis=-1, keepdims=True)
        expvals = jnp.exp(scores - highest)
        totals = jnp.sum(expvals, axis=-1, keepdims=True)
        attn_probs = (expvals / totals).astype(jnp.bfloat16)
        outs = jnp.einsum("hqk,khd->qhd", attn_probs, values_v, preferred_element_type=jnp.float32)
        return (outs, highest[..., 0] + jnp.log(totals[..., 0]))

    starts = jnp.arange(span // block_rows) * block_rows
    outs, log_totals = lax.map(one_block, starts)
    return (outs.reshape(span, queries.shape[1], queries.shape[2]), log_totals)


def attend_back(queries, keys_rot, values_v, grad_out, log_totals, length):
    span = queries.shape[0]
    block_rows = min(512, span)
    scale = queries.shape[2] ** (-0.5)
    starts = jnp.arange(span // block_rows) * block_rows

    def one_block(carry, item):
        first_row, lse_block = item
        rows_q = lax.dynamic_slice_in_dim(queries, first_row, block_rows, 0)
        rows_g = lax.dynamic_slice_in_dim(grad_out, first_row, block_rows, 0)
        scores = (
            jnp.einsum("qhd,khd->hqk", rows_q, keys_rot, preferred_element_type=jnp.float32) * scale
        )
        allowed = allowed_mask(first_row, block_rows, span, length)[None]
        attn_probs = jnp.where(allowed, jnp.exp(scores - lse_block[..., None]), 0.0)
        probs_low = attn_probs.astype(jnp.bfloat16)
        grad_values = carry[1] + jnp.einsum(
            "hqk,qhd->khd", probs_low, rows_g, preferred_element_type=jnp.float32
        )
        grad_probs = jnp.einsum(
            "qhd,khd->hqk", rows_g, values_v, preferred_element_type=jnp.float32
        )
        inner = jnp.sum(attn_probs * grad_probs, axis=-1, keepdims=True)
        grad_scores = (attn_probs * (grad_probs - inner)).astype(jnp.bfloat16)
        grad_rows = (
            jnp.einsum("hqk,khd->qhd", grad_scores, keys_rot, preferred_element_type=jnp.float32)
            * scale
        )
        grad_keys = (
            carry[0]
            + jnp.einsum("hqk,qhd->khd", grad_scores, rows_q, preferred_element_type=jnp.float32)
            * scale
        )
        return ((grad_keys, grad_values), grad_rows)

    zeros_kv = jnp.zeros(keys_rot.shape, jnp.float32)
    (grad_keys, grad_values), grad_rows = lax.scan(
        one_block, (zeros_kv, zeros_kv), (starts, log_totals)
    )
    return (grad_rows.reshape(queries.shape), grad_keys, grad_values)


def advance(weight, moment, average, grad, rate):
    moment_new = MOMENT * moment + grad
    weight_new = weight - rate * (grad + MOMENT * moment_new)
    average_new = KEEP * average + (1.0 - KEEP) * weight_new
    return (weight_new, moment_new, average_new)


def on_device(
    tokens,
    targets,
    lengths,
    w_qkv,
    w_out,
    w_gateup,
    w_down,
    mom_qkv,
    mom_out,
    mom_gateup,
    mom_down,
    avg_qkv,
    avg_out,
    avg_gateup,
    avg_down,
):
    n_shards = lax.axis_size("seq")
    shard_index = lax.axis_index("seq")
    member = lax.axis_index("fsdp")
    own_rows = tokens.shape[1]
    span = own_rows * n_shards
    head_size = HD
    heads_here = w_qkv.shape[2] // head_size
    inputs = tokens[0].astype(jnp.float32)
    target = targets[0].astype(jnp.float32)
    own_length = lax.dynamic_index_in_dim(lengths, member, 0, keepdims=False)
    count = jnp.sum(lengths).astype(jnp.float32)
    own_pos = shard_index * own_rows + jnp.arange(own_rows, dtype=jnp.int32)
    valid = (own_pos < own_length).astype(jnp.float32)[:, None]
    low_weights = (
        w_qkv.astype(jnp.bfloat16),
        w_out.astype(jnp.bfloat16),
        w_gateup.astype(jnp.bfloat16),
        w_down.astype(jnp.bfloat16),
    )
    full_qkv, full_out, full_gateup, full_down = (
        lax.all_gather(low_weights[0], "fsdp", axis=0, tiled=True),
        lax.all_gather(low_weights[1], "fsdp", axis=1, tiled=True),
        lax.all_gather(low_weights[2], "fsdp", axis=0, tiled=True),
        lax.all_gather(low_weights[3], "fsdp", axis=1, tiled=True),
    )
    normed_one, factor_one = layer_norm(inputs)
    group_one = lax.all_gather(normed_one.astype(jnp.bfloat16), "seq", axis=0, tiled=True)
    qkv_all = jnp.einsum("td,djc->tjc", group_one, full_qkv, preferred_element_type=jnp.float32)
    cosine, sine = rotary(span, head_size)
    queries = qkv_all[:, 0].reshape(span, heads_here, head_size)
    keys_pre = qkv_all[:, 1].reshape(span, heads_here, head_size)
    queries = (queries * cosine + rotate(queries) * sine).astype(jnp.bfloat16)
    keys_rot = (keys_pre * cosine + rotate(keys_pre) * sine).astype(jnp.bfloat16)
    values_v = qkv_all[:, 2].reshape(span, heads_here, head_size).astype(jnp.bfloat16)
    attended, log_totals = attend_forward(queries, keys_rot, values_v, own_length)
    attended = attended.reshape(span, heads_here * head_size).astype(jnp.bfloat16)
    attn_term = jnp.dot(attended, full_out, preferred_element_type=jnp.float32)
    middle = inputs + lax.psum_scatter(
        attn_term.astype(jnp.bfloat16), "seq", scatter_dimension=0, tiled=True
    ).astype(jnp.float32)
    normed_two, factor_two = layer_norm(middle)
    group_two = lax.all_gather(normed_two.astype(jnp.bfloat16), "seq", axis=0, tiled=True)
    gate_up = jnp.einsum("td,djf->tjf", group_two, full_gateup, preferred_element_type=jnp.float32)
    gate = gate_up[:, 0]
    up_part = gate_up[:, 1]
    hidden = (jax.nn.silu(gate) * up_part).astype(jnp.bfloat16)
    ffn_term = jnp.dot(hidden, full_down, preferred_element_type=jnp.float32)
    result = middle + lax.psum_scatter(
        ffn_term.astype(jnp.bfloat16), "seq", scatter_dimension=0, tiled=True
    ).astype(jnp.float32)
    diff = (result - target) * valid
    loss = lax.psum(jnp.sum(diff * diff), ("seq", "fsdp")) / (2.0 * count)
    grad_result = diff / count
    full_qkv, full_out, full_gateup, full_down = (
        lax.all_gather(low_weights[0], "fsdp", axis=0, tiled=True),
        lax.all_gather(low_weights[1], "fsdp", axis=1, tiled=True),
        lax.all_gather(low_weights[2], "fsdp", axis=0, tiled=True),
        lax.all_gather(low_weights[3], "fsdp", axis=1, tiled=True),
    )
    contract_rows = (((0,), (0,)), ((), ()))
    contract_cols = (((1,), (1,)), ((), ()))
    group_dy = lax.all_gather(grad_result.astype(jnp.bfloat16), "seq", axis=0, tiled=True)
    grad_hidden = lax.dot_general(
        group_dy, full_down, contract_cols, preferred_element_type=jnp.float32
    )
    grad_down = lax.dot_general(hidden, group_dy, contract_rows, preferred_element_type=jnp.float32)
    sigma = jax.nn.sigmoid(gate)
    grad_gate = grad_hidden * up_part * sigma * (1.0 + gate * (1.0 - sigma))
    grad_up = grad_hidden * gate * sigma
    grad_gu = jnp.stack([grad_gate, grad_up], axis=1).astype(jnp.bfloat16)
    normed_grad_two = jnp.einsum(
        "tjf,djf->td", grad_gu, full_gateup, preferred_element_type=jnp.float32
    )
    grad_gateup = jnp.einsum("td,tjf->djf", group_two, grad_gu, preferred_element_type=jnp.float32)
    own_grad_two = lax.psum_scatter(
        normed_grad_two.astype(jnp.bfloat16), "seq", scatter_dimension=0, tiled=True
    ).astype(jnp.float32)
    grad_middle = grad_result + norm_back(own_grad_two, normed_two, factor_two)
    group_da = lax.all_gather(grad_middle.astype(jnp.bfloat16), "seq", axis=0, tiled=True)
    grad_att = lax.dot_general(
        group_da, full_out, contract_cols, preferred_element_type=jnp.float32
    )
    grad_att = grad_att.astype(jnp.bfloat16).reshape(span, heads_here, head_size)
    grad_out = lax.dot_general(
        attended, group_da, contract_rows, preferred_element_type=jnp.float32
    )
    grad_rows, grad_keys, grad_values = attend_back(
        queries, keys_rot, values_v, grad_att, log_totals, own_length
    )
    grad_rows = grad_rows * cosine + unrotate(grad_rows * sine)
    grad_keys = grad_keys * cosine + unrotate(grad_keys * sine)
    grad_qkv_all = jnp.stack(
        [grad_rows.reshape(span, -1), grad_keys.reshape(span, -1), grad_values.reshape(span, -1)],
        axis=1,
    ).astype(jnp.bfloat16)
    normed_grad_one = jnp.einsum(
        "tjc,djc->td", grad_qkv_all, full_qkv, preferred_element_type=jnp.float32
    )
    grad_qkv = jnp.einsum(
        "td,tjc->djc", group_one, grad_qkv_all, preferred_element_type=jnp.float32
    )
    own_grad_one = lax.psum_scatter(
        normed_grad_one.astype(jnp.bfloat16), "seq", scatter_dimension=0, tiled=True
    ).astype(jnp.float32)
    grad_inputs = grad_middle + norm_back(own_grad_one, normed_one, factor_one)
    summed_qkv, summed_out, summed_gateup, summed_down = (
        lax.psum_scatter(
            grad_qkv.astype(jnp.bfloat16), "fsdp", scatter_dimension=0, tiled=True
        ).astype(jnp.float32),
        lax.psum_scatter(
            grad_out.astype(jnp.bfloat16), "fsdp", scatter_dimension=1, tiled=True
        ).astype(jnp.float32),
        lax.psum_scatter(
            grad_gateup.astype(jnp.bfloat16), "fsdp", scatter_dimension=0, tiled=True
        ).astype(jnp.float32),
        lax.psum_scatter(
            grad_down.astype(jnp.bfloat16), "fsdp", scatter_dimension=1, tiled=True
        ).astype(jnp.float32),
    )
    new_qkv, newmom_qkv, newavg_qkv = advance(w_qkv, mom_qkv, avg_qkv, summed_qkv, 2.0)
    new_out, newmom_out, newavg_out = advance(w_out, mom_out, avg_out, summed_out, 20.0)
    new_gateup, newmom_gateup, newavg_gateup = advance(
        w_gateup, mom_gateup, avg_gateup, summed_gateup, 2.0
    )
    new_down, newmom_down, newavg_down = advance(w_down, mom_down, avg_down, summed_down, 1.0)
    return (
        result.astype(jnp.bfloat16)[None],
        grad_inputs.astype(jnp.bfloat16)[None],
        loss,
        new_qkv,
        new_out,
        new_gateup,
        new_down,
        newmom_qkv,
        newmom_out,
        newmom_gateup,
        newmom_down,
        newavg_qkv,
        newavg_out,
        newavg_gateup,
        newavg_down,
    )


def solution(mesh):
    placed = (
        P("fsdp", "seq", None),
        P("fsdp", "seq", None),
        P(),
        P("fsdp", None, "seq"),
        P("seq", "fsdp"),
        P("fsdp", None, "seq"),
        P("seq", "fsdp"),
        P("fsdp", None, "seq"),
        P("seq", "fsdp"),
        P("fsdp", None, "seq"),
        P("seq", "fsdp"),
        P("fsdp", None, "seq"),
        P("seq", "fsdp"),
        P("fsdp", None, "seq"),
        P("seq", "fsdp"),
    )
    return jax.shard_map(
        on_device,
        mesh=mesh,
        in_specs=placed,
        out_specs=(
            P("fsdp", "seq", None),
            P("fsdp", "seq", None),
            P(),
            P("fsdp", None, "seq"),
            P("seq", "fsdp"),
            P("fsdp", None, "seq"),
            P("seq", "fsdp"),
            P("fsdp", None, "seq"),
            P("seq", "fsdp"),
            P("fsdp", None, "seq"),
            P("seq", "fsdp"),
            P("fsdp", None, "seq"),
            P("seq", "fsdp"),
            P("fsdp", None, "seq"),
            P("seq", "fsdp"),
        ),
        check_vma=False,
    )
```

profile of v0, /device:TPU:0, one launch (start us, length us, event | category | flops | bytes accessed | tf_op | source)
XLA Modules:
  0.0 1588.2 jit_solution(3938071013215438621)
XLA Ops:
  19.5 30.2 %all-gather.9.cloned.1.call-done = bf16[1024,2048]{1,0:T(8,128)(2,1)} async-done(((bf16[256,2048]{1,0:T(8,128)(2,1)}), bf16[1024,2048]{1,0:T(8,128)(2,1)}) %all-gather.9.cloned.1.call-update) | async-done | bytes 4194320 | tf_op jit(solution)/shard_map/all_gather | solution.py:165
  49.7 102.1 %all-gather.11.cloned.1.call-done = bf16[2048,3,512]{0,2,1:T(8,128)(2,1)} async-done(((bf16[256,3,512]{0,2,1:T(8,128)(2,1)}), bf16[2048,3,512]{0,2,1:T(8,128)(2,1)}) %all-gather.11.cloned.1.call-update) | async-done | bytes 6291472 | tf_op jit(solution)/shard_map/all_gather | solution.py:159
  151.9 10.5 fusion.42
  173.7 3.8 slice_negate_fusion.2
  180.4 24.5 %while.29 = (s32[]{:T(128)}, bf16[2,512,4,128]{3,1,2,0:T(8,128)(2,1)}, f32[2,4,512]{2,1,0:T(4,128)S(1)}, s32[2]{0:T(128)S(1)}, s32[]{:T(128)}, /*index=5*/bf16[1...) while((s32[]{:T(128)}, ...), condition=%wide.region_5.6_spmd.clone, body=%wide.region_2.5_spmd.sunk.clone | while | flops 1099955712 | bytes 35199660 | solution.py:69
  201.1 3.7 fusion.161
  205.0 3.7 copy.65
  208.7 6.3 convolution_convert_fusion.4
  215.1 42.9 %reduce-scatter.9.cloned.1.call-done = bf16[256,2048]{1,0:T(8,128)(2,1)} async-done(((bf16[1024,2048]{1,0:T(8,128)(2,1)}), bf16[256,2048]{1,0:T(8,128)(2,1)}) %reduce-scatter.9.cloned.1.call-update) | async-done | bytes 1048592 | tf_op jit(solution)/shard_map/reduce_scatter | solution.py:176
  261.6 5.7 copy.115
  270.4 25.8 %all-gather.15.cloned.1.call-done = bf16[1024,2048]{1,0:T(8,128)(2,1)} async-done(((bf16[256,2048]{1,0:T(8,128)(2,1)}), bf16[1024,2048]{1,0:T(8,128)(2,1)}) %all-gather.15.cloned.1.call-update) | async-done | bytes 4194320 | tf_op jit(solution)/shard_map/all_gather | solution.py:180
  296.2 229.9 %all-gather.17.cloned.1.call-done = bf16[2048,2,2048]{2,0,1:T(8,128)(2,1)} async-done(((bf16[256,2,2048]{2,0,1:T(8,128)(2,1)}), bf16[2048,2,2048]{2,0,1:T(8,128)(2,1)}) %all-gather.17.cloned.1.call-update) | async-done | bytes 16777232 | tf_op jit(solution)/shard_map/all_gather | solution.py:161
  526.1 21.5 %fusion.39 = f32[1024,2,2048]{2,0,1:T(8,128)S(1)} fusion(bf16[2048,2,2048]{2,0,1:T(8,128)(2,1)} %all-gather.17.cloned.1.call-done, bf16[1024,2048]{1,0:T(8,128)(2,1)} %all-gather.15.cloned.1.call-done), kind=kOutput, calls=%fused_computation.67 | convolution fusion | flops 17179869184 | bytes 37748736 | tf_op jit(solution)/shard_map/td,djf->tjf/dot_general | solution.py:181
  547.6 5.8 copy-done.16
  553.3 3.9 multiply_convert_fusion.3
  557.2 94.6 %all-gather.19.cloned.1.call-done = bf16[2048,2048]{1,0:T(8,128)(2,1)} async-done(((bf16[2048,256]{1,0:T(8,128)(2,1)}), bf16[2048,2048]{1,0:T(8,128)(2,1)}) %all-gather.19.cloned.1.call-update) | async-done | bytes 8388624 | tf_op jit(solution)/shard_map/all_gather | solution.py:162
  651.9 13.8 convolution_convert_fusion.3
  668.2 40.4 %reduce-scatter.11.cloned.1.call-done = bf16[256,2048]{1,0:T(8,128)(2,1)} async-done(((bf16[1024,2048]{1,0:T(8,128)(2,1)}), bf16[256,2048]{1,0:T(8,128)(2,1)}) %reduce-scatter.11.cloned.1.call-update) | async-done | bytes 1048592 | tf_op jit(solution)/shard_map/reduce_scatter | solution.py:186
  711.7 34.6 %all-gather.21.cloned.1.call-done = bf16[1024,2048]{1,0:T(8,128)(2,1)} async-done(((bf16[256,2048]{1,0:T(8,128)(2,1)}), bf16[1024,2048]{1,0:T(8,128)(2,1)}) %all-gather.21.cloned.1.call-update) | async-done | bytes 4194320 | tf_op jit(solution)/shard_map/all_gather | solution.py:200
  746.2 20.5 %fusion.46 = (bf16[1024,1,2048]{2,0,1:T(8,128)(2,1)}, bf16[1024,1,2048]{2,0,1:T(8,128)(2,1)}) fusion(f32[1024,2,2048]{2,0,1:T(8,128)} %copy-done.16, bf16[1024,2048]{1,0:T(8,128)(2,1)} %all-gather.21.cloned.1.call-done, bf16[2048,2048]{1,0:T(8,128)(2,1)} %all-gather.19.cloned.1.call-done), kind=kOutput, calls=%fused_computation.76 | convolution fusion | flops 8617197568 | bytes 37748736 | tf_op jit(solution)/shard_map/dot_general | solution.py:201
  766.7 23.9 %bitcast_convert_fusion.1 = bf16[1024,2048]{1,0:T(8,128)(2,1)} fusion(bf16[2048,2,2048]{2,0,1:T(8,128)(2,1)} %all-gather.17.cloned.1.call-done, bf16[1024,1,2048]{2,0,1:T(8,128)(2,1)} %get-tuple-element.287, bf16[1024,1,2048]{2,0,1:T(8,128)(2,1)} %get-tuple-element.286), kind=kOutput, calls=%fused_computation.54 | convolution fusion | flops 17186160640 | bytes 29360128 | tf_op jit(solution)/shard_map/tjf,djf->td/dot_general | solution.py:209
  790.7 44.7 %reduce-scatter.13.cloned.1.call-done = bf16[256,2048]{1,0:T(8,128)(2,1)} async-done(((bf16[1024,2048]{1,0:T(8,128)(2,1)}), bf16[256,2048]{1,0:T(8,128)(2,1)}) %reduce-scatter.13.cloned.1.call-update) | async-done | bytes 1048592 | tf_op jit(solution)/shard_map/reduce_scatter | solution.py:213
  835.4 3.8 multiply_reduce_fusion.1
  842.8 14.5 convolution_convert_fusion.1
  863.2 14.2 all-gather.23.cloned.1.call-done
  877.4 5.9 convolution_convert_fusion.5
  883.4 6.3 convolution_convert_fusion.6
  889.7 52.0 %while.30 = (s32[]{:T(128)}, f32[1024,4,128]{0,2,1:T(8,128)S(1)}, f32[1024,4,128]{0,2,1:T(8,128)}, f32[2,512,4,128]{3,1,2,0:T(8,128)}, s32[2]{0:T(128)S(1)}, /*i...) while((s32[]{:T(128)}, f32[1024,4,128]{0,2,1:T(8,128)S(1)}, ...), condition=%wide.region_16.17_spmd.clone.clone, body=%wide.region_14.16_spmd.clone.sunk.clone | while | flops 2719743488 | bytes 180419536 | solution.py:109
  900.3 3.7 multiply_convert_fusion.6
  904.0 3.8 bitcast_add_fusion.6
  911.3 3.9 bitcast_add_fusion.7
  925.7 3.7 multiply_convert_fusion.6
  929.4 3.8 bitcast_add_fusion.6
  936.6 5.1 bitcast_add_fusion.7
  972.9 11.0 bitcast_convert_fusion
  985.4 11.4 convolution_convert_fusion.2
  996.9 24.7 %convolution_convert_fusion = bf16[2048,2,2048]{2,0,1:T(8,128)(2,1)} fusion(bf16[1024,1,2048]{2,0,1:T(8,128)(2,1)} %get-tuple-element.287, bf16[1024,1,2048]{2,0,1:T(8,128)(2,1)} %get-tuple-element.286, bf16[1024,2048]{1,0:T(8,128)(2,1)} %all-gather.15.cloned.1.call-done), kind=kOutput, calls=%fused_computation.49 | convolution fusion | flops 17205035008 | bytes 29360128 | tf_op jit(solution)/shard_map/td,tjf->djf/dot_general | solution.py:212
  1021.7 40.7 %psum.7 = f32[]{:T(128)} all-reduce(f32[]{:T(128)} %get-tuple-element.226), channel_id=1, replica_groups=mesh['seq'=4,'fsdp'=8] {'seq','fsdp'}, use_global_device_ids=true, to_apply=%region_21.22 | all-reduce | flops 1 | bytes 8 | tf_op jit(solution)/shard_map/psum | solution.py:190
  1063.0 5.8 multiply_add_fusion
  1068.9 31.1 %reduce-scatter.19.cloned.1.call-done = bf16[512,256]{1,0:T(8,128)(2,1)} async-done(((bf16[512,2048]{1,0:T(8,128)(2,1)}), bf16[512,256]{1,0:T(8,128)(2,1)}) %reduce-scatter.19.cloned.1.call-update) | async-done | bytes 262160 | tf_op jit(solution)/shard_map/reduce_scatter | solution.py:248
  1102.6 43.9 %reduce-scatter.15.cloned.1.call-done = bf16[256,2048]{1,0:T(8,128)(2,1)} async-done(((bf16[1024,2048]{1,0:T(8,128)(2,1)}), bf16[256,2048]{1,0:T(8,128)(2,1)}) %reduce-scatter.15.cloned.1.call-update) | async-done | bytes 1048592 | tf_op jit(solution)/shard_map/reduce_scatter | solution.py:240
  1150.4 118.1 %reduce-scatter.17.cloned.1.call-done = bf16[256,3,512]{2,0,1:T(8,128)(2,1)} async-done(((bf16[2048,3,512]{2,0,1:T(8,128)(2,1)}), bf16[256,3,512]{2,0,1:T(8,128)(2,1)}) %reduce-scatter.17.cloned.1.call-update) | async-done | bytes 786448 | tf_op jit(solution)/shard_map/reduce_scatter | solution.py:245
  1268.4 5.5 multiply_add_fusion.1
  1273.9 276.9 %reduce-scatter.21.cloned.1.call-done = bf16[256,2,2048]{2,0,1:T(8,128)(2,1)} async-done(((bf16[2048,2,2048]{2,0,1:T(8,128)(2,1)}), bf16[256,2,2048]{2,0,1:T(8,128)(2,1)}) %reduce-scatter.21.cloned.1.call-update) | async-done | bytes 2097168 | tf_op jit(solution)/shard_map/reduce_scatter | solution.py:251
  1550.8 13.7 fusion.44
  1564.6 5.2 copy.83
  1569.8 5.2 copy.84
  1575.1 5.2 copy.85
  (238 shorter events, 127.1 us)
Async XLA Ops:
  7.2 3.9 copy-start.5
  7.2 42.5 %all-gather.9.cloned.1.call-start = ((), (), s32[]{:S(2)}) async-start(), calls=%async_computation.8 | async-start | bytes 5242880 | tf_op jit(solution)/shard_map/all_gather | solution.py:165
  12.4 139.5 %all-gather.11.cloned.1.call-start = ((), (), s32[]{:S(2)}) async-start(), calls=%async_computation.9 | async-start | bytes 7077888 | tf_op jit(solution)/shard_map/all_gather | solution.py:159
  13.6 195.1 %all-gather.13.cloned.1.call-start = ((), (), s32[]{:S(2)}) async-start(), calls=%async_computation.10 | async-start | bytes 2359296 | tf_op jit(solution)/shard_map/all_gather | solution.py:160
  14.5 243.5 %reduce-scatter.9.cloned.1.call-start = ((), (), s32[]{:S(2)}) async-start(), calls=%async_computation.11 | async-start | bytes 5242880 | tf_op jit(solution)/shard_map/reduce_scatter | solution.py:176
  14.5 4.4 copy-start.45
  167.8 5.9 copy-start.13
  173.7 3.8 copy-start.23
  173.7 3.8 copy-start.29
  204.9 10.1 copy-start.3
  204.9 10.1 copy-start.9
  204.9 10.0 copy-start.39
  205.0 10.0 copy-start.47
  215.0 81.1 %all-gather.15.cloned.1.call-start = ((), (), s32[]{:S(2)}) async-start(), calls=%async_computation.12 | async-start | bytes 5242880 | tf_op jit(solution)/shard_map/all_gather | solution.py:180
  261.6 264.5 %all-gather.17.cloned.1.call-start = ((), (), s32[]{:S(2)}) async-start(), calls=%async_computation.13 | async-start | bytes 18874368 | tf_op jit(solution)/shard_map/all_gather | solution.py:161
  267.4 384.5 %all-gather.19.cloned.1.call-start = ((), (), s32[]{:S(2)}) async-start(), calls=%async_computation.14 | async-start | bytes 9437184 | tf_op jit(solution)/shard_map/all_gather | solution.py:162
  270.3 438.2 %reduce-scatter.11.cloned.1.call-start = ((), (), s32[]{:S(2)}) async-start(), calls=%async_computation.15 | async-start | bytes 5242880 | tf_op jit(solution)/shard_map/reduce_scatter | solution.py:186
  547.5 5.8 copy-start.16
  665.6 42.9 %copy-start.17 = (bf16[1,256,2048]{2,1,0:T(8,128)(2,1)S(1)}, bf16[1,256,2048]{2,1,0:T(8,128)(2,1)}, u32[]{:S(2)}) copy-start(bf16[1,256,2048]{2,1,0:T(8,128)(2,1)} %param.20) | copy-start | bytes 3145732
  665.7 80.6 %all-gather.21.cloned.1.call-start = ((), (), s32[]{:S(2)}) async-start(), calls=%async_computation.16 | async-start | bytes 5242880 | tf_op jit(solution)/shard_map/all_gather | solution.py:200
  711.6 123.8 %reduce-scatter.13.cloned.1.call-start = ((), (), s32[]{:S(2)}) async-start(), calls=%async_computation.17 | async-start | bytes 5242880 | tf_op jit(solution)/shard_map/reduce_scatter | solution.py:213
  790.6 86.7 %all-gather.23.cloned.1.call-start = ((), (), s32[]{:S(2)}) async-start(), calls=%async_computation.18 | async-start | bytes 5242880 | tf_op jit(solution)/shard_map/all_gather | solution.py:217
  835.4 3.8 copy-start.18
  835.4 3.8 copy-start.31
  842.7 220.3 %reduce-scatter.23.cloned.1.call-start = ((), (), s32[]{:S(2)}) async-start(), calls=%async_computation.23 | async-start | bytes 9437184 | tf_op jit(solution)/shard_map/reduce_scatter | solution.py:254
  857.3 242.6 %reduce-scatter.19.cloned.1.call-start = ((), (), s32[]{:S(2)}) async-start(), calls=%async_computation.21 | async-start | bytes 2359296 | tf_op jit(solution)/shard_map/reduce_scatter | solution.py:248
  860.0 17.3 %copy-start.34 = (bf16[2,512,4,128]{3,2,1,0:T(4,128)(2,1)S(1)}, bf16[2,512,4,128]{3,2,1,0:T(4,128)(2,1)}, u32[]{:S(2)}) copy-start(bf16[2,512,4,128]{3,2,1,0:T(4,128)(2,1)} %copy.65) | copy-start | bytes 3145732
  883.3 6.3 copy-start.4
  883.3 6.3 copy-start.40
  883.3 6.3 copy-start.48
  883.3 263.2 %reduce-scatter.15.cloned.1.call-start = ((), (), s32[]{:S(2)}) async-start(), calls=%async_computation.19 | async-start | bytes 5242880 | tf_op jit(solution)/shard_map/reduce_scatter | solution.py:240
  892.4 4.3 copy-start.11
  892.4 4.3 copy-start.26
  894.9 5.4 copy-start
  904.0 3.8 copy-start.2
  904.0 6.5 copy-start.1
  917.7 4.3 copy-start.11
  917.7 4.3 copy-start.26
  920.2 5.4 copy-start
  929.4 3.8 copy-start.2
  929.4 6.2 copy-start.1
  983.9 284.5 %reduce-scatter.17.cloned.1.call-start = ((), (), s32[]{:S(2)}) async-start(), calls=%async_computation.20 | async-start | bytes 7077888 | tf_op jit(solution)/shard_map/reduce_scatter | solution.py:245
  996.9 553.9 %reduce-scatter.21.cloned.1.call-start = ((), (), s32[]{:S(2)}) async-start(), calls=%async_computation.22 | async-start | bytes 18874368 | tf_op jit(solution)/shard_map/reduce_scatter | solution.py:251
  1021.7 41.4 %copy-start.21 = (f32[2048,256]{1,0:T(8,128)S(1)}, f32[2048,256]{1,0:T(8,128)}, u32[]{:S(2)}) copy-start(f32[2048,256]{1,0:T(8,128)} %param.25) | copy-start | bytes 6291460
  1068.9 77.7 %copy-start.6 = (bf16[1,256,2048]{2,1,0:T(8,128)(2,1)S(1)}, bf16[1,256,2048]{2,1,0:T(8,128)(2,1)}, u32[]{:S(2)}) copy-start(bf16[1,256,2048]{2,1,0:T(8,128)(2,1)} %param.19) | copy-start | bytes 3145732
  1068.9 77.7 %copy-start.42 = (f32[256]{0:T(256)S(1)}, f32[256]{0:T(256)}, u32[]{:S(2)}) copy-start(f32[256]{0:T(256)} %copy-done.41) | copy-start | bytes 3076
  1068.9 77.7 %copy-start.44 = (f32[256]{0:T(256)S(1)}, f32[256]{0:T(256)}, u32[]{:S(2)}) copy-start(f32[256]{0:T(256)} %copy-done.43) | copy-start | bytes 3076
  1068.9 79.7 %copy-start.22 = (f32[256,2048]{1,0:T(8,128)S(1)}, f32[256,2048]{1,0:T(8,128)}, u32[]{:S(2)}) copy-start(f32[256,2048]{1,0:T(8,128)} %get-tuple-element.281) | copy-start | bytes 6291460
  (26 other events, 62.1 us)
Sparse Core Ops, SparseCore 0:
  12.5 37.1 all-gather.8
  52.3 99.4 all-gather.10
  154.5 48.5 all-gather.12
  215.2 42.7 reduce-scatter.8
  261.7 34.4 all-gather.14
  298.8 227.2 all-gather.16
  528.7 123.1 all-gather.18
  665.8 42.7 reduce-scatter.10
  711.7 34.4 all-gather.20
  790.8 44.5 reduce-scatter.12
  842.8 34.4 all-gather.22
  880.8 147.8 reduce-scatter.22
  1032.2 67.6 reduce-scatter.18
  1102.9 43.5 reduce-scatter.14
  1150.0 118.4 reduce-scatter.16
  1272.1 278.7 reduce-scatter.20
where the time goes:
time: 1590 us
  waiting for transfers between devices  1130 us (71%)
  matrix products  215 us (14%)
  other arithmetic  98.9 us (6%)
  local copies, waits for them, and re-layouts  78.1 us (5%)
  blocking collectives  40.7 us (3%)
  between operations  17.1 us (1%)
    reduce_scatter x1, waiting for transfers between devices, on_device(): lax.psum_scatter(grad_gateup.astype(jnp.bfloat16), 'fsdp', scatter_dimens...  277 us
    all_gather x1, waiting for transfers between devices, on_device(): lax.all_gather(low_weights[2], 'fsdp', axis=0, tiled=True)  230 us
    reduce_scatter x1, waiting for transfers between devices, on_device(): lax.psum_scatter(grad_qkv.astype(jnp.bfloat16), 'fsdp', scatter_dimension...  118 us
    all_gather x1, waiting for transfers between devices, on_device(): lax.all_gather(low_weights[0], 'fsdp', axis=0, tiled=True)  102 us
    all_gather x1, waiting for transfers between devices, on_device(): lax.all_gather(low_weights[3], 'fsdp', axis=1, tiled=True)  94.6 us
    reduce_scatter x1, waiting for transfers between devices, on_device(): lax.psum_scatter(normed_grad_two.astype(jnp.bfloat16), 'seq', scatter_dim...  44.7 us
    reduce_scatter x1, waiting for transfers between devices, on_device(): lax.psum_scatter(normed_grad_one.astype(jnp.bfloat16), 'seq', scatter_dim...  43.9 us
    reduce_scatter x1, waiting for transfers between devices, on_device(): lax.psum_scatter(attn_term.astype(jnp.bfloat16), 'seq', scatter_dimension...  42.9 us
  transfers between devices with their start and end apart: 16, of which 14 were waited for; matrix products, arithmetic and copies ran while one was open for 17% of the time, Pallas kernels for 0%

commit v1 on v0

--- a/solution.py
+++ b/solution.py
@@ -1,3 +1,4 @@
+import functools
 import jax
 import jax.numpy as jnp
 from jax import lax
@@ -9,6 +10,41 @@
 MOMENT = 0.9
 KEEP = 0.95
 NEG = -1e30
+
+
+def name_sections_up(local_x, dim_no):
+    local_x = jnp.moveaxis(local_x, 0, dim_no)
+    now = local_x.shape
+    return local_x.reshape(*now[:dim_no], now[dim_no] * now[dim_no + 1], *now[dim_no + 2 :])
+
+
+def review_islands(here_x, across, array_dim):
+    k_all = jax.lax.axis_size(across)
+    arrivals = []
+    c = 0
+    while c < k_all:
+        arrivals.append((c, (c + 1) % k_all))
+        c += 1
+    rows = []
+    for k0, hop_no in arrivals:
+        rows.append((hop_no, k0))
+    formed, x_next = ([], [])
+    dev = 0
+    while dev < k_all - 1:
+        if dev % 2 == 0:
+            formed.append(jax.lax.ppermute(formed[-1] if formed else here_x, across, arrivals))
+        else:
+            x_next.append(jax.lax.ppermute(x_next[-1] if x_next else here_x, across, rows))
+        dev = dev + 1
+    opened = jnp.stack([*formed[::-1], here_x, *x_next])
+    carry_out = jax.lax.axis_index(across)
+    new = len(formed)
+    part_now = carry_out - new
+    opened = opened[(jnp.arange(k_all) - part_now) % k_all]
+    return name_sections_up(opened, array_dim)
+
+
+_match_stages_all = functools.partial(review_islands, across="fsdp", array_dim=1)
 
 
 def layer_norm(values):
@@ -159,7 +195,7 @@
         lax.all_gather(low_weights[0], "fsdp", axis=0, tiled=True),
         lax.all_gather(low_weights[1], "fsdp", axis=1, tiled=True),
         lax.all_gather(low_weights[2], "fsdp", axis=0, tiled=True),
-        lax.all_gather(low_weights[3], "fsdp", axis=1, tiled=True),
+        _match_stages_all(low_weights[3]),
     )
     normed_one, factor_one = layer_norm(inputs)
     group_one = lax.all_gather(normed_one.astype(jnp.bfloat16), "seq", axis=0, tiled=True)

time: 1590 us -> 1690 us (1.063)
  waiting for transfers between devices: 1130 us -> 1180 us
  local copies, waits for them, and re-layouts: 78.1 us -> 100 us
  starting transfers between devices: 0.66 us -> 19.7 us
    ppermute x0 -> x7, waiting for transfers between devices: none -> 188 us  [the longest x4 182 us: review_islands(): jax.lax.ppermute(formed[-1] if formed else here_x, across, arrivals)]
    all_gather x1, waiting for transfers between devices: 230 us -> 89.7 us  [on_device(): lax.all_gather(low_weights[2], 'fsdp', axis=0, tiled=True)]
    all_gather x1, waiting for transfers between devices: 94.6 us -> 125 us  [on_device(): lax.all_gather(low_weights[3], 'fsdp', axis=1, tiled=True)]
    all_gather x1, waiting for transfers between devices: 25.8 us -> 0.01 us  [on_device(): lax.all_gather(normed_two.astype(jnp.bfloat16), 'seq', axis=0, tiled=True)]
    ppermute x0 -> x7, starting transfers between devices: none -> 19 us  [the longest x3 15 us: review_islands(): jax.lax.ppermute(x_next[-1] if x_next else here_x, across, rows)]
    unnamed x85 -> x101, local copies, waits for them, and re-layouts: 33 us -> 38.2 us
  transfers between devices with their start and end apart: 16 -> 23, of which waited for: 14 -> 18; matrix products, arithmetic and copies ran while one was open for 17% -> 16% of each run, Pallas kernels for 0% -> 0%
where the time goes in v1:
time: 1690 us
  waiting for transfers between devices  1180 us (70%)
  matrix products  222 us (13%)
  local copies, waits for them, and re-layouts  100 us (6%)
  other arithmetic  98.7 us (6%)
  blocking collectives  40.6 us (2%)
  starting transfers between devices  19.7 us (1%)
  between operations  17.2 us (1%)
    reduce_scatter x1, waiting for transfers between devices, on_device(): lax.psum_scatter(grad_gateup.astype(jnp.bfloat16), 'fsdp', scatter_dimens...  277 us
    ppermute x4, waiting for transfers between devices, review_islands(): jax.lax.ppermute(formed[-1] if formed else here_x, across, arrivals)  182 us
    all_gather x1, waiting for transfers between devices, on_device(): lax.all_gather(low_weights[3], 'fsdp', axis=1, tiled=True)  125 us
    reduce_scatter x1, waiting for transfers between devices, on_device(): lax.psum_scatter(grad_qkv.astype(jnp.bfloat16), 'fsdp', scatter_dimension...  117 us
    all_gather x1, waiting for transfers between devices, on_device(): lax.all_gather(low_weights[0], 'fsdp', axis=0, tiled=True)  102 us
    all_gather x1, waiting for transfers between devices, on_device(): lax.all_gather(low_weights[2], 'fsdp', axis=0, tiled=True)  89.7 us
    reduce_scatter x1, waiting for transfers between devices, on_device(): lax.psum_scatter(normed_grad_two.astype(jnp.bfloat16), 'seq', scatter_dim...  44.7 us
    reduce_scatter x1, waiting for transfers between devices, on_device(): lax.psum_scatter(normed_grad_one.astype(jnp.bfloat16), 'seq', scatter_dim...  43.9 us
  transfers between devices with their start and end apart: 23, of which 18 were waited for; matrix products, arithmetic and copies ran while one was open for 16% of the time, Pallas kernels for 0%

profile of v1, /device:TPU:0, one launch (start us, length us, event | category | flops | bytes accessed | tf_op | source)
XLA Modules:
  0.0 1687.8 jit_solution(16341686114919573871)
XLA Ops:
  20.8 30.2 %all-gather.9.cloned.1.call-done = bf16[1024,2048]{1,0:T(8,128)(2,1)} async-done(((bf16[256,2048]{1,0:T(8,128)(2,1)}), bf16[1024,2048]{1,0:T(8,128)(2,1)}) %all-gather.9.cloned.1.call-update) | async-done | bytes 4194320 | tf_op jit(solution)/shard_map/all_gather | solution.py:201
  51.0 102.1 %all-gather.11.cloned.1.call-done = bf16[2048,3,512]{0,2,1:T(8,128)(2,1)} async-done(((bf16[256,3,512]{0,2,1:T(8,128)(2,1)}), bf16[2048,3,512]{0,2,1:T(8,128)(2,1)}) %all-gather.11.cloned.1.call-update) | async-done | bytes 6291472 | tf_op jit(solution)/shard_map/all_gather | solution.py:195
  153.1 10.4 fusion.55
  170.8 5.0 slice_negate_fusion.2
  177.2 24.9 %while.29 = (s32[]{:T(128)}, bf16[2,512,4,128]{3,1,2,0:T(8,128)(2,1)}, f32[2,4,512]{2,1,0:T(4,128)S(1)}, s32[2]{0:T(128)S(1)}, s32[]{:T(128)}, /*index=5*/bf16[1...) while((s32[]{:T(128)}, ...), condition=%wide.region_5.6_spmd.clone, body=%wide.region_2.5_spmd.sunk.clone | while | flops 1099955712 | bytes 31005332 | solution.py:105
  206.0 6.3 convolution_convert_fusion.3
  212.3 42.9 %reduce-scatter.9.cloned.1.call-done = bf16[256,2048]{1,0:T(8,128)(2,1)} async-done(((bf16[1024,2048]{1,0:T(8,128)(2,1)}), bf16[256,2048]{1,0:T(8,128)(2,1)}) %reduce-scatter.9.cloned.1.call-update) | async-done | bytes 1048592 | tf_op jit(solution)/shard_map/reduce_scatter | solution.py:212
  260.1 5.7 copy.147
  269.3 26.0 %collective-permute-done = bf16[2048,256]{1,0:T(8,128)(2,1)S(1)} collective-permute-done((bf16[2048,256]{1,0:T(8,128)(2,1)S(1)}, bf16[2048,256]{1,0:T(8,128)(2,1)S(1)}, u32[]{:S(2)}, u32[]{:S(2)}) %collective-permute-start) | collective-permute-done | bytes 1048608 | tf_op jit(solution)/shard_map/ppermute | solution.py:35
  295.3 4.7 collective-permute-start.4
  300.0 62.6 %collective-permute-done.1 = bf16[2048,256]{1,0:T(8,128)(2,1)S(1)} collective-permute-done((bf16[2048,256]{1,0:T(8,128)(2,1)S(1)}, bf16[2048,256]{1,0:T(8,128)(2,1)S(1)}, u32[]{:S(2)}, u32[]{:S(2)}) %collective-permute-start.1) | collective-permute-done | bytes 1048608 | tf_op jit(solution)/shard_map/ppermute | solution.py:35
  365.1 5.1 collective-permute-start.5
  370.2 40.1 %collective-permute-done.2 = bf16[2048,256]{1,0:T(8,128)(2,1)} collective-permute-done((bf16[2048,256]{1,0:T(8,128)(2,1)S(1)}, bf16[2048,256]{1,0:T(8,128)(2,1)}, u32[]{:S(2)}, u32[]{:S(2)}) %collective-permute-start.2) | collective-permute-done | bytes 1048608 | tf_op jit(solution)/shard_map/ppermute | solution.py:35
  410.3 5.7 collective-permute-done.5
  416.0 5.2 collective-permute-start.6
  421.2 53.5 %collective-permute-done.3 = bf16[2048,256]{1,0:T(8,128)(2,1)} collective-permute-done((bf16[2048,256]{1,0:T(8,128)(2,1)}, bf16[2048,256]{1,0:T(8,128)(2,1)}, u32[]{:S(2)}, u32[]{:S(2)}) %collective-permute-start.3) | collective-permute-done | bytes 1048608 | tf_op jit(solution)/shard_map/ppermute | solution.py:35
  488.2 8.3 gather_fusion
  496.5 11.4 copy.98
  507.9 89.7 %all-gather.17.cloned.1.call-done = bf16[2048,2,2048]{2,0,1:T(8,128)(2,1)} async-done(((bf16[256,2,2048]{2,0,1:T(8,128)(2,1)}), bf16[2048,2,2048]{2,0,1:T(8,128)(2,1)}) %all-gather.17.cloned.1.call-update) | async-done | bytes 16777232 | tf_op jit(solution)/shard_map/all_gather | solution.py:197
  597.6 23.5 %fusion.52 = f32[1024,2,2048]{2,0,1:T(8,128)} fusion(bf16[2048,2,2048]{2,0,1:T(8,128)(2,1)} %all-gather.17.cloned.1.call-done, bf16[1024,2048]{1,0:T(8,128)(2,1)} %all-gather.15.cloned.1.call-done), kind=kOutput, calls=%fused_computation.81 | convolution fusion | flops 17179869184 | bytes 37748736 | tf_op jit(solution)/shard_map/td,djf->tjf/dot_general | solution.py:217
  621.0 17.5 %fusion.61 = bf16[1024,2048]{1,0:T(8,128)(2,1)} fusion(bf16[2048,2048]{0,1:T(8,128)(2,1)} %bitcast.264, f32[1024,2,2048]{2,0,1:T(8,128)} %fusion.52), kind=kOutput, calls=%fused_computation.92 | convolution fusion | flops 8604614656 | bytes 29360128 | tf_op jit(solution)/shard_map/dot_general | solution.py:221
  641.3 41.6 %reduce-scatter.11.cloned.1.call-done = bf16[256,2048]{1,0:T(8,128)(2,1)} async-done(((bf16[1024,2048]{1,0:T(8,128)(2,1)}), bf16[256,2048]{1,0:T(8,128)(2,1)}) %reduce-scatter.11.cloned.1.call-update) | async-done | bytes 1048592 | tf_op jit(solution)/shard_map/reduce_scatter | solution.py:222
  686.0 124.5 %all-gather.21.cloned.1.call-done = bf16[2048,2048]{1,0:T(8,128)(2,1)} async-done(((bf16[2048,256]{1,0:T(8,128)(2,1)}), bf16[2048,2048]{1,0:T(8,128)(2,1)}) %all-gather.21.cloned.1.call-update) | async-done | bytes 8388624 | tf_op jit(solution)/shard_map/all_gather | solution.py:232
  810.5 34.8 %all-gather.19.cloned.1.call-done = bf16[1024,2048]{1,0:T(8,128)(2,1)} async-done(((bf16[256,2048]{1,0:T(8,128)(2,1)}), bf16[1024,2048]{1,0:T(8,128)(2,1)}) %all-gather.19.cloned.1.call-update) | async-done | bytes 4194320 | tf_op jit(solution)/shard_map/all_gather | solution.py:236
  845.4 20.5 %fusion.60 = (bf16[1024,1,2048]{2,0,1:T(8,128)(2,1)}, bf16[1024,1,2048]{2,0,1:T(8,128)(2,1)}) fusion(f32[1024,2,2048]{2,0,1:T(8,128)} %fusion.52, bf16[1024,2048]{1,0:T(8,128)(2,1)} %all-gather.19.cloned.1.call-done, bf16[2048,2048]{1,0:T(8,128)(2,1)} %all-gather.21.cloned.1.call-done), kind=kOutput, calls=%fused_computation.90 | convolution fusion | flops 8617197568 | bytes 37748736 | tf_op jit(solution)/shard_map/dot_general | solution.py:237
  865.9 23.8 %bitcast_convert_fusion.1 = bf16[1024,2048]{1,0:T(8,128)(2,1)} fusion(bf16[2048,2,2048]{2,0,1:T(8,128)(2,1)} %all-gather.17.cloned.1.call-done, bf16[1024,1,2048]{2,0,1:T(8,128)(2,1)} %get-tuple-element.321, bf16[1024,1,2048]{2,0,1:T(8,128)(2,1)} %get-tuple-element.320), kind=kOutput, calls=%fused_computation.53 | convolution fusion | flops 17186160640 | bytes 29360128 | tf_op jit(solution)/shard_map/tjf,djf->td/dot_general | solution.py:245
  889.7 44.7 %reduce-scatter.13.cloned.1.call-done = bf16[256,2048]{1,0:T(8,128)(2,1)} async-done(((bf16[1024,2048]{1,0:T(8,128)(2,1)}), bf16[256,2048]{1,0:T(8,128)(2,1)}) %reduce-scatter.13.cloned.1.call-update) | async-done | bytes 1048592 | tf_op jit(solution)/shard_map/reduce_scatter | solution.py:249
  941.8 16.6 convolution_convert_fusion.1
  964.2 12.1 all-gather.23.cloned.1.call-done
  976.4 5.9 convolution_convert_fusion.4
  982.4 6.3 convolution_convert_fusion.5
  988.6 52.2 %while.30 = (s32[]{:T(128)}, f32[1024,4,128]{0,2,1:T(8,128)S(1)}, f32[1024,4,128]{0,2,1:T(8,128)}, f32[2,512,4,128]{3,1,2,0:T(8,128)}, s32[2]{0:T(128)S(1)}, /*i...) while((s32[]{:T(128)}, f32[1024,4,128]{0,2,1:T(8,128)S(1)}, ...), condition=%wide.region_16.17_spmd.clone.clone, body=%wide.region_14.16_spmd.clone.sunk.clone | while | flops 2719743488 | bytes 180419536 | solution.py:145
  1010.3 3.9 bitcast_add_fusion.7
  1035.7 5.1 bitcast_add_fusion.7
  1072.0 11.0 bitcast_convert_fusion
  1084.5 11.4 convolution_convert_fusion.2
  1096.1 24.7 %convolution_convert_fusion = bf16[2048,2,2048]{2,0,1:T(8,128)(2,1)} fusion(bf16[1024,1,2048]{2,0,1:T(8,128)(2,1)} %get-tuple-element.321, bf16[1024,1,2048]{2,0,1:T(8,128)(2,1)} %get-tuple-element.320, bf16[1024,2048]{1,0:T(8,128)(2,1)} %all-gather.15.cloned.1.call-done), kind=kOutput, calls=%fused_computation.50 | convolution fusion | flops 17205035008 | bytes 29360128 | tf_op jit(solution)/shard_map/td,tjf->djf/dot_general | solution.py:248
  1120.8 40.6 %psum.7 = f32[]{:T(128)} all-reduce(f32[]{:T(128)} %get-tuple-element.260), channel_id=1, replica_groups=mesh['seq'=4,'fsdp'=8] {'seq','fsdp'}, use_global_device_ids=true, to_apply=%region_21.22 | all-reduce | flops 1 | bytes 8 | tf_op jit(solution)/shard_map/psum | solution.py:226
  1162.1 5.8 multiply_add_fusion
  1167.9 31.7 %reduce-scatter.19.cloned.1.call-done = bf16[512,256]{1,0:T(8,128)(2,1)} async-done(((bf16[512,2048]{1,0:T(8,128)(2,1)}), bf16[512,256]{1,0:T(8,128)(2,1)}) %reduce-scatter.19.cloned.1.call-update) | async-done | bytes 262160 | tf_op jit(solution)/shard_map/reduce_scatter | solution.py:284
  1202.3 43.9 %reduce-scatter.15.cloned.1.call-done = bf16[256,2048]{1,0:T(8,128)(2,1)} async-done(((bf16[1024,2048]{1,0:T(8,128)(2,1)}), bf16[256,2048]{1,0:T(8,128)(2,1)}) %reduce-scatter.15.cloned.1.call-update) | async-done | bytes 1048592 | tf_op jit(solution)/shard_map/reduce_scatter | solution.py:276
  1251.2 117.0 %reduce-scatter.17.cloned.1.call-done = bf16[256,3,512]{2,0,1:T(8,128)(2,1)} async-done(((bf16[2048,3,512]{2,0,1:T(8,128)(2,1)}), bf16[256,3,512]{2,0,1:T(8,128)(2,1)}) %reduce-scatter.17.cloned.1.call-update) | async-done | bytes 786448 | tf_op jit(solution)/shard_map/reduce_scatter | solution.py:281
  1368.1 5.5 multiply_add_fusion.1
  1373.6 276.9 %reduce-scatter.21.cloned.1.call-done = bf16[256,2,2048]{2,0,1:T(8,128)(2,1)} async-done(((bf16[2048,2,2048]{2,0,1:T(8,128)(2,1)}), bf16[256,2,2048]{2,0,1:T(8,128)(2,1)}) %reduce-scatter.21.cloned.1.call-update) | async-done | bytes 2097168 | tf_op jit(solution)/shard_map/reduce_scatter | solution.py:287
  1650.4 13.7 fusion.57
  1664.2 5.2 copy.115
  1669.4 5.2 copy.116
  1674.7 5.2 copy.117
  (269 shorter events, 168.6 us)
Async XLA Ops:
  7.2 6.5 copy-start.28
  7.2 43.8 %all-gather.9.cloned.1.call-start = ((), (), s32[]{:S(2)}) async-start(), calls=%async_computation.8 | async-start | bytes 5242880 | tf_op jit(solution)/shard_map/all_gather | solution.py:201
  13.7 139.5 %all-gather.11.cloned.1.call-start = ((), (), s32[]{:S(2)}) async-start(), calls=%async_computation.9 | async-start | bytes 7077888 | tf_op jit(solution)/shard_map/all_gather | solution.py:195
  14.9 191.1 %all-gather.13.cloned.1.call-start = ((), (), s32[]{:S(2)}) async-start(), calls=%async_computation.10 | async-start | bytes 2359296 | tf_op jit(solution)/shard_map/all_gather | solution.py:196
  15.7 239.5 %reduce-scatter.9.cloned.1.call-start = ((), (), s32[]{:S(2)}) async-start(), calls=%async_computation.11 | async-start | bytes 5242880 | tf_op jit(solution)/shard_map/reduce_scatter | solution.py:212
  202.1 10.1 copy-start.3
  202.1 10.1 copy-start.10
  202.1 10.1 copy-start.43
  202.1 10.1 copy-start.51
  212.3 43.0 %copy-start.5 = (bf16[1,256,2048]{2,1,0:T(8,128)(2,1)S(1)}, bf16[1,256,2048]{2,1,0:T(8,128)(2,1)}, u32[]{:S(2)}) copy-start(bf16[1,256,2048]{2,1,0:T(8,128)(2,1)} %param.19) | copy-start | bytes 3145732
  212.3 295.6 %all-gather.15.cloned.1.call-start = ((), (), s32[]{:S(2)}) async-start(), calls=%async_computation.12 | async-start | bytes 5242880 | tf_op jit(solution)/shard_map/all_gather | solution.py:216
  260.0 337.5 %all-gather.17.cloned.1.call-start = ((), (), s32[]{:S(2)}) async-start(), calls=%async_computation.13 | async-start | bytes 18874368 | tf_op jit(solution)/shard_map/all_gather | solution.py:197
  265.9 417.1 %reduce-scatter.11.cloned.1.call-start = ((), (), s32[]{:S(2)}) async-start(), calls=%async_computation.14 | async-start | bytes 5242880 | tf_op jit(solution)/shard_map/reduce_scatter | solution.py:222
  267.8 212.6 %copy-start.31 = (bf16[2048,256]{1,0:T(8,128)(2,1)}, bf16[2048,256]{1,0:T(8,128)(2,1)S(1)}, u32[]{:S(2)}) copy-start(bf16[2048,256]{1,0:T(8,128)(2,1)S(1)} %convert_element_type.154) | copy-start | bytes 3145732
  267.8 27.5 %collective-permute-start = (bf16[2048,256]{1,0:T(8,128)(2,1)S(1)}, bf16[2048,256]{1,0:T(8,128)(2,1)S(1)}, u32[]{:S(2)}, u32[]{:S(2)}) collective-permute-start(bf16[2048,256]{1,0:T(8,128)(2,1)S(1)} %convert_element_type.154), channel_id=1, source_target_pairs={{0,1},{1,2},{2,3},{3,4},{4,5},{5,6},{6,7},{7,0},{8,9},{9,10},{10,1... | collective-permute-start | bytes 3145736 | tf_op jit(solution)/shard_map/ppermute | solution.py:35
  295.3 69.8 %copy-start.35 = (bf16[2048,256]{1,0:T(8,128)(2,1)}, bf16[2048,256]{1,0:T(8,128)(2,1)S(1)}, u32[]{:S(2)}) copy-start(bf16[2048,256]{1,0:T(8,128)(2,1)S(1)} %collective-permute-done) | copy-start | bytes 3145732
  295.3 67.3 %collective-permute-start.1 = (bf16[2048,256]{1,0:T(8,128)(2,1)S(1)}, bf16[2048,256]{1,0:T(8,128)(2,1)S(1)}, u32[]{:S(2)}, u32[]{:S(2)}) collective-permute-start(bf16[2048,256]{1,0:T(8,128)(2,1)S(1)} %collective-permute-done), channel_id=1, source_target_pairs={{0,1},{1,2},{2,3},{3,4},{4,5},{5,6},{6,7},{7,0},{8,9},{9,10},{10,1... | collective-permute-start | bytes 3145736 | tf_op jit(solution)/shard_map/ppermute | solution.py:35
  295.3 69.8 %collective-permute-start.4 = (bf16[2048,256]{1,0:T(8,128)(2,1)S(1)}, bf16[2048,256]{1,0:T(8,128)(2,1)}, u32[]{:S(2)}, u32[]{:S(2)}) collective-permute-start(bf16[2048,256]{1,0:T(8,128)(2,1)S(1)} %convert_element_type.154), channel_id=1, source_target_pairs={{1,0},{2,1},{3,2},{4,3},{5,4},{6,5},{7,6},{0,7},{9,8},{10,9},{11,1... | collective-permute-start | bytes 3145736 | tf_op jit(solution)/shard_map/ppermute | solution.py:37
  362.6 7.6 copy-start.37
  362.6 47.7 %collective-permute-start.2 = (bf16[2048,256]{1,0:T(8,128)(2,1)S(1)}, bf16[2048,256]{1,0:T(8,128)(2,1)}, u32[]{:S(2)}, u32[]{:S(2)}) collective-permute-start(bf16[2048,256]{1,0:T(8,128)(2,1)S(1)} %collective-permute-done.1), channel_id=1, source_target_pairs={{0,1},{1,2},{2,3},{3,4},{4,5},{5,6},{6,7},{7,0},{8,9},{9,10},{10,1... | collective-permute-start | bytes 3145736 | tf_op jit(solution)/shard_map/ppermute | solution.py:35
  365.1 50.9 %collective-permute-start.5 = (bf16[2048,256]{1,0:T(8,128)(2,1)}, bf16[2048,256]{1,0:T(8,128)(2,1)}, u32[]{:S(2)}, u32[]{:S(2)}) collective-permute-start(bf16[2048,256]{1,0:T(8,128)(2,1)} %collective-permute-done.4), channel_id=1, source_target_pairs={{1,0},{2,1},{3,2},{4,3},{5,4},{6,5},{7,6},{0,7},{9,8},{10,9},{11,1... | collective-permute-start | bytes 3145736 | tf_op jit(solution)/shard_map/ppermute | solution.py:37
  410.3 64.4 %collective-permute-start.3 = (bf16[2048,256]{1,0:T(8,128)(2,1)}, bf16[2048,256]{1,0:T(8,128)(2,1)}, u32[]{:S(2)}, u32[]{:S(2)}) collective-permute-start(bf16[2048,256]{1,0:T(8,128)(2,1)} %collective-permute-done.2), channel_id=1, source_target_pairs={{0,1},{1,2},{2,3},{3,4},{4,5},{5,6},{6,7},{7,0},{8,9},{9,10},{10,1... | collective-permute-start | bytes 3145736 | tf_op jit(solution)/shard_map/ppermute | solution.py:35
  410.3 69.0 %copy-start.38 = (bf16[2048,256]{1,0:T(8,128)(2,1)S(1)}, bf16[2048,256]{1,0:T(8,128)(2,1)}, u32[]{:S(2)}) copy-start(bf16[2048,256]{1,0:T(8,128)(2,1)} %copy-done.37) | copy-start | bytes 3145732
  410.3 70.1 %copy-start.36 = (bf16[2048,256]{1,0:T(8,128)(2,1)S(1)}, bf16[2048,256]{1,0:T(8,128)(2,1)}, u32[]{:S(2)}) copy-start(bf16[2048,256]{1,0:T(8,128)(2,1)} %copy-done.35) | copy-start | bytes 3145732
  416.0 71.2 %collective-permute-start.6 = (bf16[2048,256]{1,0:T(8,128)(2,1)}, bf16[2048,256]{1,0:T(8,128)(2,1)S(1)}, u32[]{:S(2)}, u32[]{:S(2)}) collective-permute-start(bf16[2048,256]{1,0:T(8,128)(2,1)} %collective-permute-done.5), channel_id=1, source_target_pairs={{1,0},{2,1},{3,2},{4,3},{5,4},{6,5},{7,6},{0,7},{9,8},{10,9},{11,1... | collective-permute-start | bytes 3145736 | tf_op jit(solution)/shard_map/ppermute | solution.py:37
  638.5 44.4 %copy-start.18 = (bf16[1,256,2048]{2,1,0:T(8,128)(2,1)S(1)}, bf16[1,256,2048]{2,1,0:T(8,128)(2,1)}, u32[]{:S(2)}) copy-start(bf16[1,256,2048]{2,1,0:T(8,128)(2,1)} %param.20) | copy-start | bytes 3145732
  638.5 172.0 %all-gather.21.cloned.1.call-start = ((), (), s32[]{:S(2)}) async-start(), calls=%async_computation.16 | async-start | bytes 9437184 | tf_op jit(solution)/shard_map/all_gather | solution.py:232
  639.3 206.1 %all-gather.19.cloned.1.call-start = ((), (), s32[]{:S(2)}) async-start(), calls=%async_computation.15 | async-start | bytes 5242880 | tf_op jit(solution)/shard_map/all_gather | solution.py:236
  686.0 248.4 %reduce-scatter.13.cloned.1.call-start = ((), (), s32[]{:S(2)}) async-start(), calls=%async_computation.17 | async-start | bytes 5242880 | tf_op jit(solution)/shard_map/reduce_scatter | solution.py:249
  889.7 86.7 %all-gather.23.cloned.1.call-start = ((), (), s32[]{:S(2)}) async-start(), calls=%async_computation.18 | async-start | bytes 5242880 | tf_op jit(solution)/shard_map/all_gather | solution.py:253
  941.8 220.3 %reduce-scatter.23.cloned.1.call-start = ((), (), s32[]{:S(2)}) async-start(), calls=%async_computation.23 | async-start | bytes 9437184 | tf_op jit(solution)/shard_map/reduce_scatter | solution.py:290
  958.4 241.2 %reduce-scatter.19.cloned.1.call-start = ((), (), s32[]{:S(2)}) async-start(), calls=%async_computation.21 | async-start | bytes 2359296 | tf_op jit(solution)/shard_map/reduce_scatter | solution.py:284
  961.1 15.3 copy-start.34
  982.3 6.3 copy-start.4
  982.3 6.3 copy-start.44
  982.3 6.3 copy-start.52
  982.3 263.9 %reduce-scatter.15.cloned.1.call-start = ((), (), s32[]{:S(2)}) async-start(), calls=%async_computation.19 | async-start | bytes 5242880 | tf_op jit(solution)/shard_map/reduce_scatter | solution.py:276
  993.8 5.5 copy-start
  1003.1 6.5 copy-start.1
  1019.3 5.5 copy-start
  1028.5 6.2 copy-start.1
  1083.0 285.1 %reduce-scatter.17.cloned.1.call-start = ((), (), s32[]{:S(2)}) async-start(), calls=%async_computation.20 | async-start | bytes 7077888 | tf_op jit(solution)/shard_map/reduce_scatter | solution.py:281
  1096.0 554.4 %reduce-scatter.21.cloned.1.call-start = ((), (), s32[]{:S(2)}) async-start(), calls=%async_computation.22 | async-start | bytes 18874368 | tf_op jit(solution)/shard_map/reduce_scatter | solution.py:287
  1120.8 41.3 %copy-start.17 = (f32[2048,256]{1,0:T(8,128)S(1)}, f32[2048,256]{1,0:T(8,128)}, u32[]{:S(2)}) copy-start(f32[2048,256]{1,0:T(8,128)} %param.25) | copy-start | bytes 6291460
  1167.9 78.3 %copy-start.6 = (bf16[1,256,2048]{2,1,0:T(8,128)(2,1)S(1)}, bf16[1,256,2048]{2,1,0:T(8,128)(2,1)}, u32[]{:S(2)}) copy-start(bf16[1,256,2048]{2,1,0:T(8,128)(2,1)} %param.19) | copy-start | bytes 3145732
  1167.9 78.3 %copy-start.46 = (f32[256]{0:T(256)S(1)}, f32[256]{0:T(256)}, u32[]{:S(2)}) copy-start(f32[256]{0:T(256)} %copy-done.45) | copy-start | bytes 3076
  1167.9 78.3 %copy-start.48 = (f32[256]{0:T(256)S(1)}, f32[256]{0:T(256)}, u32[]{:S(2)}) copy-start(f32[256]{0:T(256)} %copy-done.47) | copy-start | bytes 3076
  1167.9 80.2 %copy-start.22 = (f32[256,2048]{1,0:T(8,128)S(1)}, f32[256,2048]{1,0:T(8,128)}, u32[]{:S(2)}) copy-start(f32[256,2048]{1,0:T(8,128)} %get-tuple-element.315) | copy-start | bytes 6291460
  (36 other events, 118.9 us)
Sparse Core Ops, SparseCore 0:
  13.8 37.1 all-gather.8
  53.6 99.4 all-gather.10
  155.7 48.5 all-gather.12
  212.4 42.7 reduce-scatter.8
  260.2 34.4 all-gather.14
  297.3 300.2 all-gather.16
  638.6 44.2 reduce-scatter.10
  685.6 124.9 all-gather.20
  812.7 32.6 all-gather.18
  889.8 44.5 reduce-scatter.12
  941.9 34.4 all-gather.22
  979.9 147.8 reduce-scatter.22
  1131.3 68.2 reduce-scatter.18
  1202.6 43.5 reduce-scatter.14
  1249.7 118.4 reduce-scatter.16
  1371.7 278.6 reduce-scatter.20
